TPU v7x, 32 devices: a whole 2x2x4 slice. The times are simulated.
32 devices in a mesh: group: 8 (over z, x), tensor: 4 (over y, core).
Axes of the slice: x: 2, y: 2, z: 4, core: 2. Of those that a mesh axis runs over, the one named last changes fastest.
Arguments:
- queries: bfloat16 [1024, 4096], P('group', 'tensor'), may hold values from -120 to 120
- keys: bfloat16 [1024, 512], P('group', 'tensor'), may hold values from -6 to 6
- values: bfloat16 [1024, 512], P('group', 'tensor'), may hold values from -6 to 6
- document_index: int32 [8, 128], P('group'), may hold values from 0 to 7, never falling along the last dimension, each value on 1 to 64 neighbouring positions
- out_proj: bfloat16 [4096, 4096], P('tensor', 'group'), may hold values from -0.25 to 0.25
- residual_in: bfloat16 [1024, 4096], P(('group', 'tensor')), may hold values from -60 to 60
- norm_gain: float32 [4096], replicated, may hold values from 0.1 to 1.9
- expert_ids: int32 [1024, 8], P(('group', 'tensor')), may hold values from 0 to 31, all different within a row; in each aligned block of 32 rows (0 to 31, 32 to 63, ...) at most 16 rows name the same one
- gate_weights: float32 [1024, 8], P(('group', 'tensor')), may hold values from 0.05 to 0.45
- w_gate_up: bfloat16 [32, 4096, 1536], P(('group', 'tensor')), may hold values from -0.09375 to 0.09375
- w_down: bfloat16 [32, 768, 4096], P(('group', 'tensor')), may hold values from -0.21875 to 0.21875
Outputs:
- layer_out: bfloat16 [1024, 4096], P(('group', 'tensor'))
Inputs may be any that keep to these rules, and one draw needn't show every extreme that they name: `document_index`: ids never fall along a group's tokens; equal ids mark one document. `expert_ids`: a token names 8 different experts; among the 32 tokens of one device (aligned blocks of rows) no expert is named more than 16 times, a bound that some block reaches.
All inputs are finite; a program needn't handle non-finite values.
Results may differ from a plain program's by a relative error of at most 0.0045.
Values may be sent and summed in bfloat16 or wider, within the bound.
A program may use at most 128 MiB of HBM per device.

v0:
```python
import jax
import jax.numpy as jnp
from jax import lax
from jax.sharding import PartitionSpec as P

HEAD_SIZE = 128


def on_device(
    queries,
    keys,
    values,
    document_index,
    out_proj,
    residual_in,
    norm_gain,
    expert_ids,
    gate_weights,
    w_gate_up,
    w_down,
):
    token_group = queries.shape[0]
    kv_dev = keys.shape[1] // HEAD_SIZE
    query_dev = queries.shape[1] // HEAD_SIZE
    group_ratio = query_dev // kv_dev
    model_width = residual_in.shape[1]
    query_head_split = queries.reshape(token_group, kv_dev, group_ratio, HEAD_SIZE)
    key_head_split = keys.reshape(token_group, kv_dev, HEAD_SIZE)
    value_head_split = values.reshape(token_group, kv_dev, HEAD_SIZE)
    scores = jnp.einsum(
        "qgrd,kgd->grqk", query_head_split, key_head_split, preferred_element_type=jnp.float32
    ) * (1.0 / HEAD_SIZE**0.5)
    doc_row = document_index[0]
    positions = jnp.arange(token_group, dtype=jnp.int32)
    visible = (positions[:, None] >= positions[None, :]) & (doc_row[:, None] == doc_row[None, :])
    scores = jnp.where(visible, scores, -jnp.inf)
    row_max = jnp.max(scores, axis=-1, keepdims=True)
    exponent = jnp.where(visible, jnp.exp(scores - row_max), 0.0)
    weights = (exponent / jnp.sum(exponent, axis=-1, keepdims=True)).astype(jnp.bfloat16)
    head_out = jnp.einsum(
        "grqk,kgd->qgrd", weights, value_head_split, preferred_element_type=jnp.float32
    )
    head_out = head_out.astype(jnp.bfloat16).reshape(token_group, query_dev * HEAD_SIZE)
    partial_value = jnp.dot(
        head_out,
        lax.all_gather(out_proj, "group", axis=1, tiled=True),
        preferred_element_type=jnp.float32,
    )
    attended = lax.psum_scatter(partial_value, "tensor", scatter_dimension=0, tiled=True)
    hidden = residual_in.astype(jnp.float32) + attended
    mean_square = jnp.mean(hidden * hidden, axis=-1, keepdims=True)
    normed = (hidden * lax.rsqrt(mean_square + 1e-06) * norm_gain).astype(jnp.bfloat16)
    tok_dev, top_count = expert_ids.shape
    experts = lax.axis_size("group") * lax.axis_size("tensor")
    capacity = 2 * tok_dev * top_count // experts
    flat_ids = expert_ids.reshape(-1)
    matches = (flat_ids[:, None] == jnp.arange(experts, dtype=jnp.int32)[None, :]).astype(jnp.int32)
    before = jnp.cumsum(matches, axis=0) - matches
    position = jnp.sum(before * matches, axis=1)
    slot_index = flat_ids * capacity + position
    slot_rows = jnp.arange(experts * capacity, dtype=jnp.int32)
    routing_table = jnp.any(
        slot_rows[:, None, None] == slot_index.reshape(1, tok_dev, top_count), axis=-1
    )
    outgoing = jnp.dot(
        routing_table.astype(jnp.bfloat16), normed, preferred_element_type=jnp.float32
    )
    outgoing = outgoing.astype(jnp.bfloat16).reshape(experts, capacity, model_width)
    gate_up = w_gate_up[0]
    down_rows = w_down[0]
    ff_width = down_rows.shape[0]
    block = lax.all_to_all(outgoing, ("group", "tensor"), split_axis=0, concat_axis=0, tiled=True)
    flat_rows = block.reshape(-1, model_width)
    projected = jnp.dot(flat_rows, gate_up, preferred_element_type=jnp.float32)
    activated = (jax.nn.silu(projected[:, :ff_width]) * projected[:, ff_width:]).astype(
        jnp.bfloat16
    )
    expert_out = jnp.dot(activated, down_rows, preferred_element_type=jnp.float32).astype(
        jnp.bfloat16
    )
    results = lax.all_to_all(
        expert_out.reshape(block.shape),
        ("group", "tensor"),
        split_axis=0,
        concat_axis=0,
        tiled=True,
    )
    results = results.reshape(experts * capacity, model_width)
    picked = results[slot_index].astype(jnp.float32).reshape(tok_dev, top_count, model_width)
    expert_sum = jnp.sum(picked * gate_weights[:, :, None], axis=1)
    return (hidden + expert_sum).astype(jnp.bfloat16)


def solution(mesh):
    in_specs = (
        P("group", "tensor"),
        P("group", "tensor"),
        P("group", "tensor"),
        P("group", None),
        P("tensor", "group"),
        P(("group", "tensor"), None),
        P(),
        P(("group", "tensor"), None),
        P(("group", "tensor"), None),
        P(("group", "tensor"), None, None),
        P(("group", "tensor"), None, None),
    )
    out_specs = P(("group", "tensor"), None)
    return jax.shard_map(
        on_device, mesh=mesh, in_specs=in_specs, out_specs=out_specs, check_vma=False
    )
```

profile of v0, /device:TPU:0, one launch (start us, length us, event | category | flops | bytes accessed | tf_op | source)
XLA Modules:
  0.0 402.8 jit_solution(7738283838798815911)
XLA Ops:
  6.5 0.0 copy-start
  6.5 0.7 all-gather.2.cloned.1.call-update
  7.3 0.0 reduce-scatter.2.cloned.1.call-start
  7.3 0.8 fusion.21
  8.1 1.0 fusion.31
  9.1 0.1 fusion.14
  9.3 1.0 convolution_convert_fusion.1
  10.3 126.8 %all-gather.2.cloned.1.call-done = bf16[1024,4096]{1,0:T(8,128)(2,1)} async-done(((bf16[1024,512]{1,0:T(8,128)(2,1)}), bf16[1024,4096]{1,0:T(8,128)(2,1)}) %all-gather.2.cloned.1.call-update) | async-done | bytes 8388624 | tf_op jit(solution)/shard_map/all_gather | solution.py:46
  137.1 6.1 %fusion.32 = f32[128,4096]{1,0:T(8,128)} fusion(bf16[128,1024]{0,1:T(8,128)(2,1)S(1)} %bitcast.77, bf16[1024,4096]{1,0:T(8,128)(2,1)} %all-gather.2.cloned.1.call-done), kind=kOutput, calls=%fused_computation.52 | convolution fusion | flops 1073741824 | bytes 10747904 | tf_op jit(solution)/shard_map/dot_general | solution.py:44
  143.2 0.0 reduce-scatter.2.cloned.1.call-update
  143.2 0.1 copy.28
  143.3 0.1 eq.62
  143.4 0.1 eq.58
  143.5 0.6 reduce-window.6
  144.1 0.2 slice_reduce_fusion
  144.3 0.1 fusion.24
  144.4 0.1 reduce_sum.42
  144.5 0.2 fusion.13
  144.8 28.0 %reduce-scatter.2.cloned.1.call-done = f32[32,4096]{1,0:T(8,128)} async-done(((f32[128,4096]{1,0:T(8,128)}), f32[32,4096]{1,0:T(8,128)}) %reduce-scatter.2.cloned.1.call-update) | async-done | bytes 524304 | tf_op jit(solution)/shard_map/reduce_scatter | solution.py:49
  172.7 1.2 multiply_reduce_fusion
  174.0 2.4 convolution_convert_fusion
  176.3 0.0 slice-start
  176.3 98.0 %all_to_all.10 = bf16[32,16,4096]{2,1,0:T(8,128)(2,1)S(1)} all-to-all(bf16[32,16,4096]{2,1,0:T(8,128)(2,1)S(1)} %bitcast.74), channel_id=1, replica_groups=mesh['group'=8,'tensor'=4] {'group','tensor'}, dimensions={0} | all-to-all | bytes 8388608 | tf_op jit(solution)/shard_map/all_to_all | solution.py:72
  274.4 9.4 %fusion = f32[512,1536]{1,0:T(8,128)S(1)} fusion(bf16[512,4096]{1,0:T(8,128)(2,1)S(1)} %bitcast.76, bf16[1,4096,1536]{2,1,0:T(8,128)(2,1)} %param.20), kind=kOutput, calls=%fused_computation.1 | convolution fusion | flops 6442450944 | bytes 19922944 | tf_op jit(solution)/shard_map/dot_general | solution.py:74
  283.8 5.0 %fusion.4 = bf16[512,4096]{1,0:T(8,128)(2,1)} fusion(bf16[1,768,4096]{2,1,0:T(8,128)(2,1)S(1)} %bitcast.82, f32[512,1536]{1,0:T(8,128)S(1)} %fusion), kind=kOutput, calls=%fused_computation.5 | convolution fusion | flops 3225681920 | bytes 13631488 | tf_op jit(solution)/shard_map/dot_general | solution.py:78
  288.8 4.0 all-to-all-start.1
  292.8 0.1 mul.81
  292.9 0.1 copy.32
  293.0 93.9 %all-to-all-done.1 = bf16[32,16,4096]{2,1,0:T(8,128)(2,1)} async-done(((bf16[32,16,4096]{2,1,0:T(8,128)(2,1)}), bf16[32,16,4096]{2,1,0:T(8,128)(2,1)}, u32[]{:S(2)}, u32[]{:S(2)}) %all-to-all-start.1) | async-done | bytes 4194336 | tf_op jit(solution)/shard_map/all_to_all | solution.py:81
  386.8 6.7 %gather_fusion = bf16[256,4096]{1,0:T(8,128)(2,1)S(1)} fusion(bf16[512,4096]{1,0:T(8,128)(2,1)} %bitcast.16, s32[1024]{0:T(1024)S(1)} %pad_clamp_fusion), kind=kCustom, calls=%fused_computation | custom fusion | bytes 4195328 | tf_op jit(solution)/shard_map/gather | solution.py:89
  393.5 1.6 fusion.7
  395.2 0.8 add_convert_fusion
  (23 shorter events, 0.1 us)
Async XLA Ops:
  6.5 1.6 copy-start
  6.5 130.5 %all-gather.2.cloned.1.call-start = ((), (), s32[]{:S(2)}) async-start(), calls=%async_computation.3 | async-start | bytes 9437184 | tf_op jit(solution)/shard_map/all_gather | solution.py:46
  7.3 165.5 %reduce-scatter.2.cloned.1.call-start = ((), (), s32[]{:S(2)}) async-start(), calls=%async_computation.4 | async-start | bytes 2621440 | tf_op jit(solution)/shard_map/reduce_scatter | solution.py:49
  137.1 6.1 %copy-start.4 = (s32[32,8]{0,1:T(8,128)S(1)}, s32[32,8]{0,1:T(8,128)}, u32[]{:S(2)}) copy-start(s32[32,8]{0,1:T(8,128)} %param.18) | copy-start | bytes 3076
  137.1 35.7 %copy-start.2 = (bf16[32,4096]{1,0:T(8,128)(2,1)S(1)}, bf16[32,4096]{1,0:T(8,128)(2,1)}, u32[]{:S(2)}) copy-start(bf16[32,4096]{1,0:T(8,128)(2,1)} %param.16) | copy-start | bytes 786436
  137.1 36.9 %copy-start.3 = (f32[4096]{0:T(1024)S(1)}, f32[4096]{0:T(1024)}, u32[]{:S(2)}) copy-start(f32[4096]{0:T(1024)} %param.17) | copy-start | bytes 49156
  176.3 107.4 %slice-start = ((s8[6291456]{0:T(1024)(128)(4,1)}), s8[4194304]{0:T(1024)(128)(4,1)S(1)}, s32[]{:S(2)}) async-start(s8[6291456]{0:T(1024)(128)(4,1)} %bitcast.81), calls=%async_computation.5 | async-start | bytes 8388608
  274.4 9.4 %slice-start.1 = ((s8[6291456]{0:T(1024)(128)(4,1)}), s8[2097152]{0:T(1024)(128)(4,1)S(1)}, s32[]{:S(2)}) async-start(s8[6291456]{0:T(1024)(128)(4,1)} %bitcast.81), calls=%async_computation.6 | async-start | bytes 4194304
  288.8 4.1 %copy-start.5 = (f32[32,8]{0,1:T(8,128)S(1)}, f32[32,8]{0,1:T(8,128)}, u32[]{:S(2)}) copy-start(f32[32,8]{0,1:T(8,128)} %param.19) | copy-start | bytes 3076
  288.8 98.1 %all-to-all-start.1 = ((bf16[32,16,4096]{2,1,0:T(8,128)(2,1)}), bf16[32,16,4096]{2,1,0:T(8,128)(2,1)}, u32[]{:S(2)}, u32[]{:S(2)}) async-start(bf16[32,16,4096]{2,1,0:T(8,128)(2,1)} %bitcast.75), calls=%async_computation.2 | async-start | bytes 8388608 | tf_op jit(solution)/shard_map/all_to_all | solution.py:81
  386.8 8.3 %copy-start.1 = (f32[32,4096]{1,0:T(8,128)S(1)}, f32[32,4096]{1,0:T(8,128)}, u32[]{:S(2)}) copy-start(f32[32,4096]{1,0:T(8,128)} %reduce-scatter.2.cloned.1.call-done) | copy-start | bytes 1572868
Sparse Core Ops, SparseCore 0:
  9.4 127.6 all-gather.1
  143.3 29.3 reduce-scatter.1
where the time goes:
time: 403 us
  waiting for transfers between devices  249 us (62%)
  blocking collectives  98 us (24%)
  matrix products  24.9 us (6%)
  between operations  13.6 us (3%)
  local copies, waits for them, and re-layouts  7.38 us (2%)
  other arithmetic  5.56 us (1%)
    all_gather x1, waiting for transfers between devices, on_device(): lax.all_gather(out_proj, 'group', axis=1, tiled=True)  127 us
    all_to_all x1, blocking collectives, on_device(): lax.all_to_all(outgoing, ('group', 'tensor'), split_axis=0, concat_axis=0...  98 us
    all_to_all x1, waiting for transfers between devices, on_device(): lax.all_to_all(expert_out.reshape(block.shape), ('group', 'tensor'), spli...  93.9 us
    reduce_scatter x1, waiting for transfers between devices, on_device(): lax.psum_scatter(partial_value, 'tensor', scatter_dimension=0, tiled=True)  28 us
    dot_general x1, matrix products, on_device(): projected = jnp.dot(flat_rows, gate_up, preferred_element_type=jnp.float32)  9.35 us
  transfers between devices with their start and end apart: 3, of which 3 were waited for; matrix products, arithmetic and copies ran while one was open for 1% of the time, Pallas kernels for 0%

commit v1 on v0

v1 whole, which is shorter than its diff:
```python
import functools

import jax
import jax.numpy as jnp
from jax import lax
from jax.experimental import pallas as pl
from jax.experimental.pallas import tpu as pltpu
from jax.sharding import PartitionSpec as P

HEAD_SIZE = 128
LANES = 128


def attention(queries, keys, values, document_index):
    token_group = queries.shape[0]
    kv_dev = keys.shape[1] // HEAD_SIZE
    query_dev = queries.shape[1] // HEAD_SIZE
    group_ratio = query_dev // kv_dev
    query_head_split = queries.reshape(token_group, kv_dev, group_ratio, HEAD_SIZE)
    key_head_split = keys.reshape(token_group, kv_dev, HEAD_SIZE)
    value_head_split = values.reshape(token_group, kv_dev, HEAD_SIZE)
    scores = jnp.einsum(
        "qgrd,kgd->grqk", query_head_split, key_head_split, preferred_element_type=jnp.float32
    ) * (1.0 / HEAD_SIZE**0.5)
    doc_row = document_index[0]
    positions = jnp.arange(token_group, dtype=jnp.int32)
    visible = (positions[:, None] >= positions[None, :]) & (doc_row[:, None] == doc_row[None, :])
    scores = jnp.where(visible, scores, -jnp.inf)
    row_max = jnp.max(scores, axis=-1, keepdims=True)
    exponent = jnp.where(visible, jnp.exp(scores - row_max), 0.0)
    weights = (exponent / jnp.sum(exponent, axis=-1, keepdims=True)).astype(jnp.bfloat16)
    head_out = jnp.einsum(
        "grqk,kgd->qgrd", weights, value_head_split, preferred_element_type=jnp.float32
    )
    return head_out.astype(jnp.bfloat16).reshape(token_group, query_dev * HEAD_SIZE)


MESH = pl.DeviceIdType.MESH
VMEM_LIMIT = 60 * 1024 * 1024


def place(sizes):
    g, t = lax.axis_index("group"), lax.axis_index("tensor")
    return g // 2, g % 2, t // 2, t % 2


def device(z, x, y, c):
    return (z * 2 + x, y * 2 + c)


def enter(partners):
    barrier = pltpu.get_barrier_semaphore()
    for partner in partners:
        pl.semaphore_signal(barrier, inc=1, device_id=partner, device_id_type=MESH)
    pl.semaphore_wait(barrier, len(partners))


def remote(src, dst, send, recv, target):
    return pltpu.make_async_remote_copy(
        src_ref=src,
        dst_ref=dst,
        send_sem=send,
        recv_sem=recv,
        device_id=target,
        device_id_type=MESH,
    )


def project_kernel(
    slabs,
    head_ref,
    w_ref,
    out_ref,
    heads,
    part,
    got_core,
    sum_core,
    got_y,
    sum_y,
    landed,
    z_send,
    z_recv,
    x_send,
    x_recv,
    c_send,
    c_recv,
    y_send,
    y_recv,
    o_send,
    o_recv,
):
    z, x, y, c = place(None)
    width = w_ref.shape[1]
    tok = out_ref.shape[0]
    after = [lax.rem(z + j, slabs) for j in range(slabs)]
    before = [lax.rem(z + slabs - j, slabs) for j in range(slabs)]
    core, over_y, over_x = device(z, x, y, 1 - c), device(z, x, 1 - y, c), device(z, 1 - x, y, c)
    enter(
        [core, over_y]
        + [device(after[j], x, y, c) for j in range(1, slabs)]
        + [device(after[j], 1 - x, y, c) for j in range(slabs)]
    )
    pending = []

    def start(copy):
        copy.start()
        pending.append(copy)
        return copy

    z_copy = [None] * slabs
    x_copy = [None] * slabs
    x_copy[0] = start(remote(head_ref, heads.at[0, 1], x_send.at[0], x_recv.at[0], over_x))
    for j in range(1, slabs):
        z_copy[j] = start(
            remote(
                head_ref, heads.at[j, 0], z_send.at[j], z_recv.at[j], device(before[j], x, y, c)
            )
        )
    c_copy, y_copy, o_copy = [None] * slabs, [None] * slabs, []

    def project(j):
        for side in range(2):
            rows = head_ref if j == 0 and side == 0 else heads.at[j, side]
            got = jnp.dot(rows[...], w_ref[...], preferred_element_type=jnp.float32)
            part[j, :, side] = got.reshape(2, 2, tok, width).transpose(1, 0, 2, 3)
        c_copy[j] = start(
            remote(part.at[j, 1 - c], got_core.at[j], c_send.at[j], c_recv.at[j], core)
        )

    def over_cores(j):
        c_copy[j].wait_recv()
        for side in range(2):
            for row in range(2):
                sum_core[j, row, side] = part[j, c, side, row] + got_core[j, side, row]
        y_copy[j] = start(
            remote(sum_core.at[j, 1 - y], got_y.at[j], y_send.at[j], y_recv.at[j], over_y)
        )

    def over_rows(j):
        y_copy[j].wait_recv()
        for side in range(2):
            total = (sum_core[j, y, side] + got_y[j, side]).astype(jnp.bfloat16)
            if j == 0 and side == 0:
                landed[0, 0] = total
                continue
            sum_y[j, side] = total
            target = device(after[j], x if side == 0 else 1 - x, y, c)
            o_copy.append(
                start(
                    remote(
                        sum_y.at[j, side],
                        landed.at[j, side],
                        o_send.at[j, side],
                        o_recv.at[j, side],
                        target,
                    )
                )
            )

    for j in range(slabs):
        if j + 1 < slabs:
            z_copy[j + 1].wait_recv()
            x_copy[j + 1] = start(
                remote(
                    heads.at[j + 1, 0],
                    heads.at[j + 1, 1],
                    x_send.at[j + 1],
                    x_recv.at[j + 1],
                    over_x,
                )
            )
        x_copy[j].wait_recv()
        project(j)
        if j >= 1:
            over_cores(j - 1)
        if j >= 2:
            over_rows(j - 2)
    over_cores(slabs - 1)
    for j in range(max(slabs - 2, 0), slabs):
        over_rows(j)
    for copy in o_copy:
        copy.wait_recv()
    for copy in pending:
        copy.wait_send()
    for j in range(slabs):
        for side in range(2):
            owner = before[j] * 2 + (x if side == 0 else 1 - x)
            columns = pl.ds(pl.multiple_of(owner * width, width), width)
            out_ref[:, columns] = landed[j, side].astype(jnp.float32)


def project(head_out, out_proj, groups, tok_dev):
    slabs = groups // 2
    tokens, depth = head_out.shape
    width = out_proj.shape[1]
    dma = pltpu.SemaphoreType.DMA
    return pl.pallas_call(
        functools.partial(project_kernel, slabs),
        out_shape=jax.ShapeDtypeStruct((tok_dev, groups * width), jnp.float32),
        in_specs=[pl.BlockSpec(memory_space=pltpu.VMEM)] * 2,
        out_specs=pl.BlockSpec(memory_space=pltpu.VMEM),
        scratch_shapes=[
            pltpu.VMEM((slabs, 2, tokens, depth), jnp.bfloat16),
            pltpu.VMEM((slabs, 2, 2, 2, tok_dev, width), jnp.float32),
            pltpu.VMEM((slabs, 2, 2, tok_dev, width), jnp.float32),
            pltpu.VMEM((slabs, 2, 2, tok_dev, width), jnp.float32),
            pltpu.VMEM((slabs, 2, tok_dev, width), jnp.float32),
            pltpu.VMEM((slabs, 2, tok_dev, width), jnp.bfloat16),
            pltpu.VMEM((slabs, 2, tok_dev, width), jnp.bfloat16),
        ]
        + [dma((slabs,))] * 8
        + [dma((slabs, 2))] * 2,
        compiler_params=pltpu.CompilerParams(
            collective_id=0, has_side_effects=True, vmem_limit_bytes=VMEM_LIMIT
        ),
    )(head_out, out_proj)


def combine_kernel(
    slabs,
    w_ref,
    hidden_ref,
    out_ref,
    got_core,
    sum_core,
    got_a,
    got_b,
    sum_a,
    sum_b,
    last_a,
    last_b,
    done,
    landed,
    c_send,
    c_recv,
    a_send,
    a_recv,
    b_send,
    b_recv,
    la_send,
    la_recv,
    lb_send,
    lb_recv,
    z_send,
    z_recv,
):
    z, x, y, c = place(None)
    tok, width = out_ref.shape
    half = width // 2
    step = 512
    after = [lax.rem(z + j, slabs) for j in range(slabs)]
    core, over_y, over_x = device(z, x, y, 1 - c), device(z, x, 1 - y, c), device(z, 1 - x, y, c)
    enter([core, over_y, over_x] + [device(after[j], x, y, c) for j in range(1, slabs)])
    pending = []

    def start(copy):
        copy.start()
        pending.append(copy)
        return copy

    order = [j for j in range(1, slabs)] + [0]
    c_copy = {
        j: start(
            remote(
                w_ref.at[after[j], :, :, 1 - c],
                got_core.at[j],
                c_send.at[j],
                c_recv.at[j],
                core,
            )
        )
        for j in order
    }
    a_copy, b_copy, la_copy, lb_copy, z_copy = {}, {}, {}, {}, {}

    def add(n, first, second, store):
        @pl.loop(0, n // step)
        def _(i):
            columns = pl.ds(pl.multiple_of(i * step, step), step)
            store(columns, first(columns).astype(jnp.float32) + second(columns).astype(jnp.float32))

    def over_cores(j):
        c_copy[j].wait_recv()
        for u in range(2):
            for v in range(2):

                def store(columns, value):
                    sum_core[j, u, v, :, columns] = value.astype(jnp.bfloat16)

                add(
                    width,
                    lambda columns: w_ref[after[j], u, v, c, :, columns],
                    lambda columns: got_core[j, u, v, :, columns],
                    store,
                )
        a_copy[j] = start(
            remote(
                sum_core.at[j, 1 - x, :, :, pl.ds(0, half)],
                got_a.at[j],
                a_send.at[j],
                a_recv.at[j],
                over_x,
            )
        )
        b_copy[j] = start(
            remote(
                sum_core.at[j, :, 1 - y, :, pl.ds(half, half)],
                got_b.at[j],
                b_send.at[j],
                b_recv.at[j],
                over_y,
            )
        )

    def second(j):
        a_copy[j].wait_recv()
        b_copy[j].wait_recv()
        for v in range(2):

            def store_a(columns, value):
                sum_a[j, v, :, columns] = value.astype(jnp.bfloat16)

            add(
                half,
                lambda columns: sum_core[j, x, v, :, columns],
                lambda columns: got_a[j, v, :, columns],
                store_a,
            )

            def store_b(columns, value):
                sum_b[j, v, :, columns] = value.astype(jnp.bfloat16)

            add(
                half,
                lambda columns: sum_core[
                    j, v, y, :, pl.ds(pl.multiple_of(columns.start + half, step), step)
                ],
                lambda columns: got_b[j, v, :, columns],
                store_b,
            )
        la_copy[j] = start(
            remote(sum_a.at[j, 1 - y], last_a.at[j], la_send.at[j], la_recv.at[j], over_y)
        )
        lb_copy[j] = start(
            remote(sum_b.at[j, 1 - x], last_b.at[j], lb_send.at[j], lb_recv.at[j], over_x)
        )

    def third(j):
        la_copy[j].wait_recv()
        lb_copy[j].wait_recv()

        def store_a(columns, value):
            done[j, :, columns] = value.astype(jnp.bfloat16)

        add(
            half,
            lambda columns: sum_a[j, y, :, columns],
            lambda columns: last_a[j, :, columns],
            store_a,
        )

        def store_b(columns, value):
            shifted = pl.ds(pl.multiple_of(columns.start + half, step), step)
            done[j, :, shifted] = value.astype(jnp.bfloat16)

        add(
            half,
            lambda columns: sum_b[j, x, :, columns],
            lambda columns: last_b[j, :, columns],
            store_b,
        )
        if j:
            z_copy[j] = start(
                remote(
                    done.at[j],
                    landed.at[j],
                    z_send.at[j],
                    z_recv.at[j],
                    device(after[j], x, y, c),
                )
            )

    for i, j in enumerate(order):
        over_cores(j)
        if i >= 1:
            second(order[i - 1])
        if i >= 2:
            third(order[i - 2])
    second(order[-1])
    for j in order[max(slabs - 2, 0) :]:
        third(j)
    for j in range(1, slabs):
        z_copy[j].wait_recv()
    for copy in pending:
        copy.wait_send()

    @pl.loop(0, width // step)
    def _(i):
        columns = pl.ds(pl.multiple_of(i * step, step), step)
        total = hidden_ref[:, columns] + done[0, :, columns].astype(jnp.float32)
        for j in range(1, slabs):
            total = total + landed[j, :, columns].astype(jnp.float32)
        out_ref[:, columns] = total.astype(jnp.bfloat16)


def combine(weighted, hidden, groups):
    slabs = groups // 2
    tok, width = hidden.shape
    half = width // 2
    dma = pltpu.SemaphoreType.DMA
    bf16 = jnp.bfloat16
    return pl.pallas_call(
        functools.partial(combine_kernel, slabs),
        out_shape=jax.ShapeDtypeStruct((tok, width), bf16),
        in_specs=[pl.BlockSpec(memory_space=pltpu.VMEM)] * 2,
        out_specs=pl.BlockSpec(memory_space=pltpu.VMEM),
        scratch_shapes=[
            pltpu.VMEM((slabs, 2, 2, tok, width), bf16),
            pltpu.VMEM((slabs, 2, 2, tok, width), bf16),
            pltpu.VMEM((slabs, 2, tok, half), bf16),
            pltpu.VMEM((slabs, 2, tok, half), bf16),
            pltpu.VMEM((slabs, 2, tok, half), bf16),
            pltpu.VMEM((slabs, 2, tok, half), bf16),
            pltpu.VMEM((slabs, tok, half), bf16),
            pltpu.VMEM((slabs, tok, half), bf16),
            pltpu.VMEM((slabs, tok, width), bf16),
            pltpu.VMEM((slabs, tok, width), bf16),
        ]
        + [dma((slabs,))] * 12,
        compiler_params=pltpu.CompilerParams(
            collective_id=1, has_side_effects=True, vmem_limit_bytes=VMEM_LIMIT
        ),
    )(weighted.reshape(slabs, 2, 2, 2, tok, width), hidden)


def on_device(
    queries,
    keys,
    values,
    document_index,
    out_proj,
    residual_in,
    norm_gain,
    expert_ids,
    gate_weights,
    w_gate_up,
    w_down,
):
    groups, tensors = lax.axis_size("group"), lax.axis_size("tensor")
    experts = groups * tensors
    tok_dev, model_width = residual_in.shape
    head_out = attention(queries, keys, values, document_index)
    attended = project(head_out, out_proj, groups, tok_dev)
    hidden = residual_in.astype(jnp.float32) + attended
    mean_square = jnp.mean(hidden * hidden, axis=-1, keepdims=True)
    normed = (hidden * lax.rsqrt(mean_square + 1e-06) * norm_gain).astype(jnp.bfloat16)
    gates = jnp.sum(
        jnp.where(
            expert_ids[:, :, None] == jnp.arange(experts, dtype=jnp.int32)[None, None, :],
            gate_weights[:, :, None],
            0.0,
        ),
        axis=1,
    )
    high = lax.reduce_precision(gates, 8, 7)
    low = gates - high
    pad = -(2 * experts) % LANES
    extra = jnp.concatenate(
        [high, low, jnp.zeros((tok_dev, pad), jnp.float32)], axis=1
    ).astype(jnp.bfloat16)
    rows = jnp.concatenate([normed, extra], axis=1)
    rows_all = lax.all_gather(rows, ("group", "tensor"), axis=0, tiled=True)
    me = lax.axis_index("group") * tensors + lax.axis_index("tensor")
    picked = jnp.arange(extra.shape[1], dtype=jnp.int32) % experts == me
    picked = picked & (jnp.arange(extra.shape[1], dtype=jnp.int32) < 2 * experts)
    gate_col = jnp.sum(
        jnp.where(picked[None, :], rows_all[:, model_width:].astype(jnp.float32), 0.0),
        axis=1,
        keepdims=True,
    )
    gate_up = w_gate_up[0]
    down_rows = w_down[0]
    ff_width = down_rows.shape[0]
    projected = jnp.dot(rows_all[:, :model_width], gate_up, preferred_element_type=jnp.float32)
    activated = (jax.nn.silu(projected[:, :ff_width]) * projected[:, ff_width:]).astype(
        jnp.bfloat16
    )
    expert_out = jnp.dot(activated, down_rows, preferred_element_type=jnp.float32)
    weighted = (expert_out * gate_col).astype(jnp.bfloat16)
    if weighted.size * 2 * 4 <= VMEM_LIMIT and tensors == 4:
        return combine(weighted, hidden, groups)
    expert_sum = lax.psum_scatter(weighted, ("group", "tensor"), scatter_dimension=0, tiled=True)
    return (hidden + expert_sum.astype(jnp.float32)).astype(jnp.bfloat16)


def solution(mesh):
    in_specs = (
        P("group", "tensor"),
        P("group", "tensor"),
        P("group", "tensor"),
        P("group", None),
        P("tensor", "group"),
        P(("group", "tensor"), None),
        P(),
        P(("group", "tensor"), None),
        P(("group", "tensor"), None),
        P(("group", "tensor"), None, None),
        P(("group", "tensor"), None, None),
    )
    out_specs = P(("group", "tensor"), None)
    return jax.shard_map(
        on_device, mesh=mesh, in_specs=in_specs, out_specs=out_specs, check_vma=False
    )
```

time: 403 us -> 240 us (0.60)
  waiting for transfers between devices: 249 us -> 79.5 us
  Pallas kernels: 0 us -> 108 us
  blocking collectives: 98 us -> 0 us
  matrix products: 24.9 us -> 30.2 us
    pallas_call x0 -> x2, Pallas kernels: none -> 108 us  [the longest x1 54.4 us: project(): pl.pallas_call(functools.partial(project_kernel, slabs), out_shape=jax.Sh...]
    all_to_all x1 -> x0, blocking collectives: 98 us -> none  [on_device(): lax.all_to_all(outgoing, ('group', 'tensor'), split_axis=0, concat_axis=0...]
    all_to_all x1 -> x0, waiting for transfers between devices: 93.9 us -> none  [on_device(): lax.all_to_all(expert_out.reshape(block.shape), ('group', 'tensor'), spli...]
    all_gather x1, waiting for transfers between devices: 127 us -> 79.4 us  [on_device(): rows_all = lax.all_gather(rows, ('group', 'tensor'), axis=0, tiled=True)]
    reduce_scatter x1 -> x0, waiting for transfers between devices: 28 us -> none  [on_device(): lax.psum_scatter(partial_value, 'tensor', scatter_dimension=0, tiled=True)]
    dot_general x1, matrix products: 5.03 us -> 11.8 us  [on_device(): jnp.dot(activated, down_rows, preferred_element_type=jnp.float32)]
    gather x1 -> x0, local copies, waits for them, and re-layouts: 6.67 us -> none  [on_device(): results[slot_index].astype(jnp.float32)]
    dot_general x5 -> x3, matrix products: 19.9 us -> 18.4 us  [the longest x1 16.4 us: on_device(): jnp.dot(rows_all[:, :model_width], gate_up, preferred_element_type=jnp.fl...]
  transfers between devices with their start and end apart: 3 -> 1, of which waited for: 3 -> 1; matrix products, arithmetic and copies ran while one was open for 1% -> 0% of each run, Pallas kernels for 0% -> 0%
where the time goes in v1:
time: 240 us; the launch traced here: 239 us
  Pallas kernels  108 us (45%)
  waiting for transfers between devices  79.5 us (33%)
  matrix products  30.2 us (13%)
  between operations  13.5 us (6%)
  local copies, waits for them, and re-layouts  4.88 us (2%)
  other arithmetic  3.52 us (1%)
    all_gather x1, waiting for transfers between devices, on_device(): rows_all = lax.all_gather(rows, ('group', 'tensor'), axis=0, tiled=True)  79.4 us
    pallas_call x1, Pallas kernels, project(): pl.pallas_call(functools.partial(project_kernel, slabs), out_shape=jax.Sh...  54.4 us
    pallas_call x1, Pallas kernels, combine(): pl.pallas_call(functools.partial(combine_kernel, slabs), out_shape=jax.Sh...  53.4 us
    dot_general x1, matrix products, on_device(): jnp.dot(rows_all[:, :model_width], gate_up, preferred_element_type=jnp.fl...  16.4 us
    dot_general x1, matrix products, on_device(): jnp.dot(activated, down_rows, preferred_element_type=jnp.float32)  11.8 us
  transfers between devices with their start and end apart: 1, of which 1 were waited for; matrix products, arithmetic and copies ran while one was open for 0% of the time, Pallas kernels for 0%

profile of v1, /device:TPU:0, one launch (start us, length us, event | category | flops | bytes accessed | tf_op | source)
XLA Modules:
  0.0 239.4 jit_solution(10364809159535925130)
XLA Ops:
  6.5 0.0 copy-start
  6.5 0.0 copy-start.2
  6.5 0.0 copy-start.3
  6.5 0.0 all-gather.2.cloned.1.call-start
  6.5 0.8 fusion.14
  7.4 0.8 copy.22
  8.1 0.8 copy.23
  8.9 0.1 select_reduce_fusion.1
  9.1 0.0 copy-done
  9.1 1.0 fusion.20
  10.1 0.1 fusion.9
  10.2 1.0 convolution_convert_fusion
  11.2 0.9 copy.27.head_ref
  12.1 54.4 %shard_map.109 = f32[32,4096]{1,0:T(8,128)} custom-call(bf16[128,1024]{1,0:T(8,128)(2,1)} %copy.27.head_ref, bf16[1024,512]{1,0:T(8,128)(2,1)} %w_ref.1), custom_call_target="tpu_custom_call" | custom-call | tf_op jit(solution)/shard_map/pallas_call | solution.py:197
  66.5 0.0 copy-done.2
  66.5 1.2 multiply_reduce_fusion
  67.7 0.0 copy-start.1
  67.7 0.0 copy-done.3
  67.7 0.1 multiply_convert_fusion.1
  67.8 0.8 concatenate.6
  68.7 0.0 all-gather.2.cloned.1.call-update
  68.7 79.4 %all-gather.2.cloned.1.call-done = bf16[1024,4224]{1,0:T(8,128)(2,1)} async-done(((bf16[32,4224]{1,0:T(8,128)(2,1)}), bf16[1024,4224]{1,0:T(8,128)(2,1)}) %all-gather.2.cloned.1.call-update) | async-done | bytes 8650768 | tf_op jit(solution)/shard_map/all_gather | solution.py:472
  148.1 1.1 select_reduce_fusion
  149.2 16.4 %fusion = f32[1024,1536]{1,0:T(8,128)S(1)} fusion(bf16[1,4096,1536]{2,1,0:T(8,128)(2,1)} %param.20, bf16[1024,4224]{1,0:T(8,128)(2,1)} %all-gather.2.cloned.1.call-done), kind=kOutput, calls=%fused_computation.1 | convolution fusion | flops 12884901888 | bytes 27262976 | tf_op jit(solution)/shard_map/dot_general | solution.py:484
  165.7 0.0 copy-done.1
  165.7 11.8 %multiply_convert_fusion = bf16[1024,4096]{1,0:T(8,128)(2,1)} fusion(f32[1024]{0:T(1024)S(1)} %select_reduce_fusion, bf16[1,768,4096]{2,1,0:T(8,128)(2,1)} %param.21, f32[1024,1536]{1,0:T(8,128)S(1)} %fusion), kind=kOutput, calls=%fused_computation | convolution fusion | flops 6455558144 | bytes 20975616 | tf_op jit(solution)/shard_map/dot_general | solution.py:488
  177.5 53.4 %shard_map.110 = bf16[32,4096]{1,0:T(8,128)(2,1)} custom-call(bf16[4,2,2,2,32,4096]{5,4,3,2,1,0:T(8,128)(2,1)} %bitcast.41, f32[32,4096]{1,0:T(8,128)} %copy-done.1), custom_call_target="tpu_custom_call" | custom-call | tf_op jit(solution)/shard_map/pallas_call | solution.py:412
  230.9 1.7 copy.36
  (4 shorter events, 0.0 us)
Async XLA Ops:
  6.5 2.5 %copy-start = (bf16[128,1024]{1,0:T(8,128)(2,1)S(1)}, bf16[128,1024]{1,0:T(8,128)(2,1)}, u32[]{:S(2)}) copy-start(bf16[128,1024]{1,0:T(8,128)(2,1)} %param.11) | copy-start | bytes 786436
  6.5 59.9 %copy-start.2 = (bf16[32,4096]{1,0:T(8,128)(2,1)S(1)}, bf16[32,4096]{1,0:T(8,128)(2,1)}, u32[]{:S(2)}) copy-start(bf16[32,4096]{1,0:T(8,128)(2,1)} %param.16) | copy-start | bytes 786436
  6.5 61.2 %copy-start.3 = (f32[4096]{0:T(1024)S(1)}, f32[4096]{0:T(1024)}, u32[]{:S(2)}) copy-start(f32[4096]{0:T(1024)} %param.17) | copy-start | bytes 49156
  6.5 141.6 %all-gather.2.cloned.1.call-start = ((), (), s32[]{:S(2)}) async-start(), calls=%async_computation | async-start | bytes 8921088 | tf_op jit(solution)/shard_map/all_gather | solution.py:472
  67.7 98.0 %copy-start.1 = (f32[32,4096]{1,0:T(8,128)}, f32[32,4096]{1,0:T(8,128)S(1)}, u32[]{:S(2)}) copy-start(f32[32,4096]{1,0:T(8,128)S(1)} %get-tuple-element.6.hidden_ref) | copy-start | bytes 1572868
Sparse Core Ops, SparseCore 0:
  68.8 79.2 all-gather.1

commit v2 on v1

--- a/solution.py
+++ b/solution.py
@@ -433,6 +433,83 @@
     )(weighted.reshape(slabs, 2, 2, 2, tok, width), hidden)
 
 
+def gather_kernel(slabs, half, rows_ref, out_ref, own_sem, *sems):
+    z, x, y, c = place(None)
+    width = rows_ref.shape[1]
+    low, high = pl.ds(0, half), pl.ds(half, width - half)
+    after = [lax.rem(z + j, slabs) for j in range(slabs)]
+    before = [lax.rem(z + slabs - j, slabs) for j in range(slabs)]
+    core, over_y, over_x = device(z, x, y, 1 - c), device(z, x, 1 - y, c), device(z, 1 - x, y, c)
+    own = pltpu.make_async_copy(rows_ref, out_ref.at[z, x, y, c], own_sem)
+    own.start()
+    enter([core, over_y, over_x] + [device(after[j], x, y, c) for j in range(1, slabs)])
+    copies = {}
+
+    def send(kind, j, src, dst, target):
+        copy = remote(src, dst, sems[2 * kind].at[j], sems[2 * kind + 1].at[j], target)
+        copy.start()
+        copies[kind, j] = copy
+
+    def pass_on(kind, j, block, target):
+        send(kind, j, block, block, target)
+
+    for j in range(1, slabs):
+        send(0, j, rows_ref, out_ref.at[z, x, y, c], device(before[j], x, y, c))
+
+    def first(j):
+        if j:
+            copies[0, j].wait_recv()
+        else:
+            own.wait()
+        pass_on(1, j, out_ref.at[after[j], x, y, c, :, low], over_x)
+        pass_on(2, j, out_ref.at[after[j], x, y, c, :, high], over_y)
+        pass_on(3, j, out_ref.at[after[j], x, y, c], core)
+
+    def second(j):
+        copies[1, j].wait_recv()
+        pass_on(4, j, out_ref.at[after[j], :, y, c, :, low], over_y)
+        pass_on(5, j, out_ref.at[after[j], 1 - x, y, c, :, low], core)
+        copies[2, j].wait_recv()
+        pass_on(6, j, out_ref.at[after[j], x, :, c, :, high], over_x)
+        pass_on(7, j, out_ref.at[after[j], x, 1 - y, c, :, high], core)
+
+    def third(j):
+        copies[4, j].wait_recv()
+        pass_on(8, j, out_ref.at[after[j], :, 1 - y, c, :, low], core)
+        copies[6, j].wait_recv()
+        pass_on(9, j, out_ref.at[after[j], 1 - x, :, c, :, high], core)
+
+    for j in range(slabs + 2):
+        if j < slabs:
+            first(j)
+        if 0 <= j - 1 < slabs:
+            second(j - 1)
+        if 0 <= j - 2:
+            third(j - 2)
+    for (kind, _), copy in copies.items():
+        if kind in (3, 5, 7, 8, 9):
+            copy.wait_recv()
+        copy.wait_send()
+
+
+def gather(rows, groups):
+    slabs = groups // 2
+    tok, width = rows.shape
+    half = width // LANES // 2 * LANES
+    dma = pltpu.SemaphoreType.DMA
+    out = pl.pallas_call(
+        functools.partial(gather_kernel, slabs, half),
+        out_shape=jax.ShapeDtypeStruct((slabs, 2, 2, 2, tok, width), rows.dtype),
+        in_specs=[pl.BlockSpec(memory_space=pltpu.VMEM)],
+        out_specs=pl.BlockSpec(memory_space=pltpu.VMEM),
+        scratch_shapes=[dma] + [dma((slabs,))] * 20,
+        compiler_params=pltpu.CompilerParams(
+            collective_id=2, has_side_effects=True, vmem_limit_bytes=VMEM_LIMIT // 2
+        ),
+    )(rows)
+    return out.reshape(slabs * 8 * tok, width)
+
+
 def on_device(
     queries,
     keys,
@@ -469,7 +546,11 @@
         [high, low, jnp.zeros((tok_dev, pad), jnp.float32)], axis=1
     ).astype(jnp.bfloat16)
     rows = jnp.concatenate([normed, extra], axis=1)
-    rows_all = lax.all_gather(rows, ("group", "tensor"), axis=0, tiled=True)
+    on_chip = experts * rows.size * 2 * 4 <= VMEM_LIMIT and tensors == 4
+    if on_chip:
+        rows_all = gather(rows, groups)
+    else:
+        rows_all = lax.all_gather(rows, ("group", "tensor"), axis=0, tiled=True)
     me = lax.axis_index("group") * tensors + lax.axis_index("tensor")
     picked = jnp.arange(extra.shape[1], dtype=jnp.int32) % experts == me
     picked = picked & (jnp.arange(extra.shape[1], dtype=jnp.int32) < 2 * experts)
@@ -487,7 +568,7 @@
     )
     expert_out = jnp.dot(activated, down_rows, preferred_element_type=jnp.float32)
     weighted = (expert_out * gate_col).astype(jnp.bfloat16)
-    if weighted.size * 2 * 4 <= VMEM_LIMIT and tensors == 4:
+    if on_chip:
         return combine(weighted, hidden, groups)
     expert_sum = lax.psum_scatter(weighted, ("group", "tensor"), scatter_dimension=0, tiled=True)
     return (hidden + expert_sum.astype(jnp.float32)).astype(jnp.bfloat16)

time: 240 us -> 195 us (0.81)
  waiting for transfers between devices: 79.5 us -> 0 us
  Pallas kernels: 108 us -> 161 us
  between operations: 13.5 us -> 0.18 us
  matrix products: 30.2 us -> 26.8 us
    all_gather x1 -> x0, waiting for transfers between devices: 79.4 us -> none  [on_device(): rows_all = lax.all_gather(rows, ('group', 'tensor'), axis=0, tiled=True)]
    pallas_call x0 -> x1, Pallas kernels: none -> 52.9 us  [gather(): pl.pallas_call(functools.partial(gather_kernel, slabs, half), out_shape=j...]
    dot_general x1, matrix products: 11.8 us -> 8.99 us  [on_device(): jnp.dot(activated, down_rows, preferred_element_type=jnp.float32)]
  transfers between devices with their start and end apart: 1 -> 0, of which waited for: 1 -> 0; matrix products, arithmetic and copies ran while one was open for 0% -> 0% of each run, Pallas kernels for 0% -> 0%
where the time goes in v2:
time: 195 us
  Pallas kernels  161 us (83%)
  matrix products  26.8 us (14%)
  local copies, waits for them, and re-layouts  4.17 us (2%)
  other arithmetic  2.57 us (1%)
    pallas_call x1, Pallas kernels, project(): pl.pallas_call(functools.partial(project_kernel, slabs), out_shape=jax.Sh...  54.4 us
    pallas_call x1, Pallas kernels, combine(): pl.pallas_call(functools.partial(combine_kernel, slabs), out_shape=jax.Sh...  53.6 us
    pallas_call x1, Pallas kernels, gather(): pl.pallas_call(functools.partial(gather_kernel, slabs, half), out_shape=j...  52.9 us
    dot_general x1, matrix products, on_device(): jnp.dot(rows_all[:, :model_width], gate_up, preferred_element_type=jnp.fl...  15.8 us
    dot_general x1, matrix products, on_device(): jnp.dot(activated, down_rows, preferred_element_type=jnp.float32)  8.99 us

profile of v2, /device:TPU:0, one launch (start us, length us, event | category | flops | bytes accessed | tf_op | source)
XLA Modules:
  0.0 194.6 jit_solution(9066939460488798312)
XLA Ops:
  0.0 0.0 copy-start
  0.0 0.0 copy-start.3
  0.0 0.0 copy-start.2
  0.0 0.8 fusion.14
  0.8 0.8 copy.22
  1.6 0.8 copy.23
  2.4 0.1 select_reduce_fusion.1
  2.5 0.0 copy-done
  2.5 1.0 fusion.20
  3.5 0.1 fusion.9
  3.7 1.0 convolution_convert_fusion
  4.7 0.9 copy.27.head_ref
  5.6 54.4 %shard_map.109 = f32[32,4096]{1,0:T(8,128)} custom-call(bf16[128,1024]{1,0:T(8,128)(2,1)} %copy.27.head_ref, bf16[1024,512]{1,0:T(8,128)(2,1)} %w_ref.1), custom_call_target="tpu_custom_call" | custom-call | tf_op jit(solution)/shard_map/pallas_call | solution.py:197
  59.9 0.0 copy-done.2
  60.0 1.2 multiply_reduce_fusion
  61.2 0.0 copy-start.1
  61.2 0.0 copy-done.3
  61.2 0.1 multiply_convert_fusion.1
  61.3 0.1 concatenate.6.rows_ref
  61.4 0.0 slice-start
  61.5 52.9 %shard_map.110 = bf16[4,2,2,2,32,4224]{5,4,3,2,1,0:T(8,128)(2,1)S(1)} custom-call(bf16[32,4224]{1,0:T(8,128)(2,1)S(1)} %concatenate.6.rows_ref), custom_call_target="tpu_custom_call" | custom-call | tf_op jit(solution)/shard_map/pallas_call | solution.py:500
  114.3 0.1 select_reduce_fusion
  114.5 0.0 slice-start.1
  114.5 15.8 %fusion = f32[1024,1536]{1,0:T(8,128)S(1)} fusion(bf16[1,4096,1536]{2,1,0:T(8,128)(2,1)} %param.20, bf16[1024,4224]{1,0:T(8,128)(2,1)S(1)} %bitcast.43), kind=kOutput, calls=%fused_computation.1 | convolution fusion | flops 12884901888 | bytes 27262976 | tf_op jit(solution)/shard_map/dot_general | solution.py:565
  130.3 0.0 copy-done.1
  130.3 0.0 slice-done
  130.3 0.0 slice-done.1
  130.3 9.0 %multiply_convert_fusion = bf16[1024,4096]{1,0:T(8,128)(2,1)} fusion(f32[1024]{0:T(1024)S(1)} %select_reduce_fusion, bf16[1,768,4096]{2,1,0:T(8,128)(2,1)S(1)} %bitcast.48, f32[1024,1536]{1,0:T(8,128)S(1)} %fusion), kind=kOutput, calls=%fused_computation | convolution fusion | flops 6455558144 | bytes 20975616 | tf_op jit(solution)/shard_map/dot_general | solution.py:569
  139.3 53.6 %shard_map.111 = bf16[32,4096]{1,0:T(8,128)(2,1)} custom-call(bf16[4,2,2,2,32,4096]{5,4,3,2,1,0:T(8,128)(2,1)} %bitcast.44, f32[32,4096]{1,0:T(8,128)} %copy-done.1), custom_call_target="tpu_custom_call" | custom-call | tf_op jit(solution)/shard_map/pallas_call | solution.py:412
  192.9 1.7 copy.36
  (5 shorter events, 0.0 us)
Async XLA Ops:
  0.0 2.5 %copy-start = (bf16[128,1024]{1,0:T(8,128)(2,1)S(1)}, bf16[128,1024]{1,0:T(8,128)(2,1)}, u32[]{:S(2)}) copy-start(bf16[128,1024]{1,0:T(8,128)(2,1)} %param.11) | copy-start | bytes 786436
  0.0 61.2 %copy-start.3 = (f32[4096]{0:T(1024)S(1)}, f32[4096]{0:T(1024)}, u32[]{:S(2)}) copy-start(f32[4096]{0:T(1024)} %param.17) | copy-start | bytes 49156
  0.0 59.9 %copy-start.2 = (bf16[32,4096]{1,0:T(8,128)(2,1)S(1)}, bf16[32,4096]{1,0:T(8,128)(2,1)}, u32[]{:S(2)}) copy-start(bf16[32,4096]{1,0:T(8,128)(2,1)} %param.16) | copy-start | bytes 786436
  61.2 69.1 %copy-start.1 = (f32[32,4096]{1,0:T(8,128)}, f32[32,4096]{1,0:T(8,128)S(1)}, u32[]{:S(2)}) copy-start(f32[32,4096]{1,0:T(8,128)S(1)} %get-tuple-element.6.hidden_ref) | copy-start | bytes 1572868
  61.4 68.9 %slice-start = ((s8[6291456]{0:T(1024)(128)(4,1)}), s8[4194304]{0:T(1024)(128)(4,1)S(1)}, s32[]{:S(2)}) async-start(s8[6291456]{0:T(1024)(128)(4,1)} %bitcast.47), calls=%async_computation | async-start | bytes 8388608
  114.5 15.9 %slice-start.1 = ((s8[6291456]{0:T(1024)(128)(4,1)}), s8[2097152]{0:T(1024)(128)(4,1)S(1)}, s32[]{:S(2)}) async-start(s8[6291456]{0:T(1024)(128)(4,1)} %bitcast.47), calls=%async_computation.1 | async-start | bytes 4194304
